TPU v7x, 32 devices: a whole 2x2x4 slice. The times are simulated.
32 devices in a mesh: col: 16 (over z, y, x), row: 2 (over core).
Axes of the slice: x: 2, y: 2, z: 4, core: 2. Of those that a mesh axis runs over, the one named last changes fastest.
Arguments:
- gradient: bfloat16 [4096, 16384], P('row', 'col'), may hold values from -120 to 120
- momentum: float32 [4096, 16384], P('row', 'col'), may hold values from -6 to 6
- right_factor: float32 [16384, 256], P(('col', 'row')), may hold values from -0.046875 to 0.046875
Outputs:
- momentum_next: float32 [4096, 16384], P('row', 'col')
- right_next: float32 [16384, 256], P(('col', 'row'))
- update: bfloat16 [4096, 16384], P('row', 'col')
All inputs are finite; a program needn't handle non-finite values.
Results may differ from a plain program's by a relative error of at most 0.0012.
Values sent between devices are 32-bit elements; how exact they have to be, the bound alone decides.
No kernel may reach another device: no remote copies, remote signals or barrier semaphores. Data moves between devices by JAX's collectives and lax.ppermute only.
A program may use at most 64 MiB of HBM per device.

v0:
```python
import math
import jax
import jax.numpy as jnp
from jax import lax
from jax.sharding import PartitionSpec as P

M = 4096
N = 16384
RANK = 256
EPS = 1e-06
FEEDBACK = 0.05


def body(gradient, momentum, right_factor):
    highest = lax.Precision.HIGHEST
    blend = momentum + gradient.astype(jnp.float32)
    right_block = lax.all_gather(right_factor, "row", axis=0, tiled=True)
    contract_rows = (((0,), (0,)), ((), ()))
    partial_value = jnp.dot(
        blend, right_block, precision=highest, preferred_element_type=jnp.float32
    )
    left = lax.psum(partial_value, "col")
    local_gram = lax.dot_general(
        left, left, contract_rows, precision=highest, preferred_element_type=jnp.float32
    )
    gram = lax.psum(local_gram, "row")
    lower = jnp.linalg.cholesky(gram)
    left_orth = jax.scipy.linalg.solve_triangular(lower, left.T, lower=True).T
    right_local = lax.dot_general(
        blend, left_orth, contract_rows, precision=highest, preferred_element_type=jnp.float32
    )
    share = lax.psum_scatter(right_local, "row", scatter_dimension=0, tiled=True)
    squares_right = lax.psum(jnp.sum(share * share, axis=0), ("col", "row"))
    right_norm = jnp.sqrt(squares_right + EPS)
    right_next = share / right_norm[None, :]
    right_whole = lax.all_gather(share, "row", axis=0, tiled=True)
    right_unit = right_whole / right_norm[None, :]
    contract_cols = (((1,), (1,)), ((), ()))
    feedback_term = lax.dot_general(
        left_orth, right_whole, contract_cols, precision=highest, preferred_element_type=jnp.float32
    )
    momentum_next = blend - FEEDBACK * feedback_term
    factor = math.sqrt(M * N / RANK)
    direction = lax.dot_general(
        left_orth, right_unit, contract_cols, precision=highest, preferred_element_type=jnp.float32
    )
    update = (factor * direction).astype(jnp.bfloat16)
    return (momentum_next, right_next, update)


def solution(mesh):
    placed = (P("row", "col"), P("row", "col"), P(("col", "row"), None))
    return jax.shard_map(
        body,
        mesh=mesh,
        in_specs=placed,
        out_specs=(P("row", "col"), P(("col", "row"), None), P("row", "col")),
        check_vma=False,
    )
```

profile of v0, /device:TPU:0, one launch (start us, length us, event | category | flops | bytes accessed | tf_op | source)
XLA Modules:
  0.0 361.9 jit_solution(6752334707807662119)
XLA Ops:
  7.2 0.0 all-gather.3.cloned.1.call-start
  7.2 0.7 all-gather.3.cloned.1.call-update
  7.9 0.0 all-reduce.4.cloned.1.call-start
  7.9 13.4 %all-gather.3.cloned.1.call-done = f32[1024,256]{1,0:T(8,128)} async-done(((f32[512,256]{1,0:T(8,128)}), f32[1024,256]{1,0:T(8,128)}) %all-gather.3.cloned.1.call-update) | async-done | bytes 1048592 | tf_op jit(solution)/shard_map/all_gather | solution.py:17
  21.3 11.0 %fusion.1 = f32[2048,256]{1,0:T(8,128)} fusion(f32[1024,256]{1,0:T(8,128)} %all-gather.3.cloned.1.call-done, f32[2048,1024]{1,0:T(8,128)} %param.4, bf16[2048,1024]{1,0:T(8,128)(2,1)} %param.3), kind=kOutput, calls=%fused_computation.6 | convolution fusion | flops 6446645248 | bytes 15728640 | tf_op jit(solution)/shard_map/dot_general | solution.py:19
  32.3 0.0 all-reduce.4.cloned.1.call-update
  32.3 0.0 all-reduce.6.cloned.1.call-start
  32.3 127.9 %all-reduce.4.cloned.1.call-done = f32[2048,256]{1,0:T(8,128)} async-done(((f32[2048,256]{1,0:T(8,128)}), f32[2048,256]{1,0:T(8,128)}) %all-reduce.4.cloned.1.call-update) | async-done | bytes 2097168 | tf_op jit(solution)/shard_map/psum | solution.py:22
  160.2 0.0 copy-start.2
  160.2 6.5 %fusion.16 = f32[256,256]{0,1:T(8,128)} fusion(f32[2048,256]{1,0:T(8,128)} %all-reduce.4.cloned.1.call-done), kind=kOutput, calls=%fused_computation.42 | convolution fusion | flops 1610612736 | bytes 2359296 | tf_op jit(solution)/shard_map/dot_general | solution.py:23
  166.7 0.0 all-reduce.6.cloned.1.call-update
  166.8 0.6 reduce-scatter.2.cloned.1.call-start
  167.3 17.0 %all-reduce.6.cloned.1.call-done = f32[256,256]{0,1:T(8,128)} async-done(((f32[256,256]{0,1:T(8,128)}), f32[256,256]{0,1:T(8,128)}) %all-reduce.6.cloned.1.call-update) | async-done | bytes 262160 | tf_op jit(solution)/shard_map/psum | solution.py:26
  184.4 1.1 copy.7
  185.5 1.0 fusion.6
  186.5 11.7 %cholesky.50 = f32[128,128]{1,0:T(8,128)S(1)} custom-call(f32[128,128]{1,0:T(8,128)S(1)} %cholesky.118), custom_call_target="Cholesky" | custom-call | tf_op jit(solution)/shard_map/jit(cholesky)/cholesky | solution.py:27
  198.2 9.8 %custom-call.15 = f32[1,128,128]{1,2,0:T(8,128)S(1)} custom-call(f32[1,128,128]{2,1,0:T(8,128)S(1)} %get-tuple-element.24), custom_call_target="InvertDiagBlocksLowerTriangular" | custom-call | tf_op jit(solution)/shard_map/jit(cholesky)/cholesky | solution.py:27
  208.1 0.2 constant_dynamic-update-slice_fusion.1
  208.3 0.3 convolution_subtract_fusion.1
  208.5 11.7 %cholesky.105 = f32[128,128]{1,0:T(8,128)S(1)} custom-call(f32[128,128]{1,0:T(8,128)S(1)} %convolution_subtract_fusion.1), custom_call_target="Cholesky" | custom-call | tf_op jit(solution)/shard_map/jit(cholesky)/cholesky | solution.py:27
  220.3 0.6 compare_reduce_fusion
  222.3 0.1 triangular_solve.57
  222.3 4.2 %while.1 = (s32[]{:T(128)}, f32[256,256]{1,0:T(8,128)S(1)}, s32[2,2]{1,0:T(2,128)S(1)}, f32[2,128,128]{2,1,0:T(8,128)S(1)}, s32[]{:T(128)}) while((s32[]{:T(128)}, f32[256,256]{1,0:T(8,128)S(1)}, s32[2,2]{1,0:T(2,128)S(1)}, f32[2,128,128]{2,1,0:T(8,128)S(1)}, s32[]{:T(128)}) %tuple.27), condition=%wide.while_cond, body=%wide.while_body.sunk | while | flops 2 | bytes 131189 | solution.py:28
  222.5 0.6 fusion.26
  223.1 1.4 bitcast_dynamic-update-slice_fusion.2
  224.5 0.6 fusion.26
  225.1 1.4 bitcast_dynamic-update-slice_fusion.2
  226.5 19.7 %custom-call.16 = f32[2,128,128]{1,2,0:T(8,128)S(1)} custom-call(f32[2,128,128]{2,1,0:T(8,128)S(1)} %get-tuple-element.10), custom_call_target="InvertDiagBlocksLowerTriangular" | custom-call | tf_op jit(solution)/shard_map/jit(_solve_triangular)/triangular_solve | solution.py:28
  246.2 0.0 copy-start
  246.2 0.0 copy-done.2
  246.2 1.1 fusion.2
  247.3 1.8 convolution_subtract_fusion
  249.1 1.1 fusion.8
  250.2 0.0 copy-done
  250.2 16.6 %fusion = f32[1024,256]{1,0:T(8,128)} fusion(f32[2048,1024]{1,0:T(8,128)} %param.4, bf16[2048,1024]{1,0:T(8,128)(2,1)S(1)} %copy-done, f32[128,2048]{1,0:T(8,128)S(1)} %fusion.8, f32[128,2048]{1,0:T(8,128)S(1)} %fusion.2), kind=kOutput, calls=%fused_computation.5 | convolution fusion | flops 6447169536 | bytes 15728640 | tf_op jit(solution)/shard_map/dot_general | solution.py:29
  266.8 0.0 reduce-scatter.2.cloned.1.call-update
  266.9 0.0 all-gather.5.cloned.1.call-start
  266.9 9.7 %reduce-scatter.2.cloned.1.call-done = f32[512,256]{1,0:T(8,128)} async-done(((f32[1024,256]{1,0:T(8,128)}), f32[512,256]{1,0:T(8,128)}) %reduce-scatter.2.cloned.1.call-update) | async-done | bytes 524304 | tf_op jit(solution)/shard_map/reduce_scatter | solution.py:32
  276.6 0.0 all-gather.5.cloned.1.call-update
  276.6 1.1 multiply_reduce_fusion
  277.8 40.8 %psum.23 = f32[256]{0:T(256)S(1)} all-reduce(f32[256]{0:T(256)S(1)} %multiply_reduce_fusion), channel_id=1, replica_groups=mesh['col'=16,'row'=2] {'col','row'}, use_global_device_ids=true, to_apply=%region_8.9 | all-reduce | flops 256 | bytes 2048 | tf_op jit(solution)/shard_map/psum | solution.py:33
  318.6 1.9 broadcast_divide_fusion
  320.5 0.0 all-gather.5.cloned.1.call-done
  320.5 0.0 copy-start.1
  320.5 0.0 copy-start.3
  320.5 16.1 %multiply_convert_fusion = bf16[2048,1024]{1,0:T(8,128)(2,1)} fusion(f32[128,2048]{1,0:T(8,128)S(1)} %fusion.8, f32[128,2048]{1,0:T(8,128)S(1)} %fusion.2, f32[1024,256]{1,0:T(8,128)} %all-gather.5.cloned.1.call-done, f32[256]{0:T(256)S(1)} %add_sqrt_fusion), kind=kOutput, calls=%fused_computation.2 | convolution fusion | flops 6447431680 | bytes 7341056 | tf_op jit(solution)/shard_map/dot_general | solution.py:44
  336.6 0.0 copy-done.1
  336.6 0.0 copy-done.3
  336.6 18.4 %multiply_subtract_fusion = f32[2048,1024]{1,0:T(8,128)} fusion(f32[1024,256]{1,0:T(8,128)S(1)} %copy-done.3, f32[2048,1024]{1,0:T(8,128)} %param.4, bf16[2048,1024]{1,0:T(8,128)(2,1)S(1)} %copy-done.1, f32[128,2048]{1,0:T(8,128)S(1)} %fusion.8, f32[128,2048]{1,0:T(8,128)S(1)} %fusion.2), kind=kOutput, calls=%fused_computation.3 | convolution fusion | flops 6451363840 | bytes 24117248 | tf_op jit(solution)/shard_map/dot_general | solution.py:39
  (10 shorter events, 0.2 us)
Async XLA Ops:
  7.2 14.1 %all-gather.3.cloned.1.call-start = ((), (), s32[]{:S(2)}) async-start(), calls=%async_computation.1 | async-start | bytes 1572864 | tf_op jit(solution)/shard_map/all_gather | solution.py:17
  7.9 152.3 %all-reduce.4.cloned.1.call-start = ((), (), s32[]{:S(2)}) async-start(), calls=%async_computation.2 | async-start | bytes 4194304 | tf_op jit(solution)/shard_map/psum | solution.py:22
  32.3 152.1 %all-reduce.6.cloned.1.call-start = ((), (), s32[]{:S(2)}) async-start(), calls=%async_computation.3 | async-start | bytes 524288 | tf_op jit(solution)/shard_map/psum | solution.py:26
  160.2 86.0 %copy-start.2 = (f32[2048,256]{1,0:T(8,128)S(1)}, f32[2048,256]{1,0:T(8,128)}, u32[]{:S(2)}) copy-start(f32[2048,256]{1,0:T(8,128)} %all-reduce.4.cloned.1.call-done) | copy-start | bytes 6291460
  166.8 109.9 %reduce-scatter.2.cloned.1.call-start = ((), (), s32[]{:S(2)}) async-start(), calls=%async_computation.4 | async-start | bytes 1572864 | tf_op jit(solution)/shard_map/reduce_scatter | solution.py:32
  246.2 4.0 %copy-start = (bf16[2048,1024]{1,0:T(8,128)(2,1)S(1)}, bf16[2048,1024]{1,0:T(8,128)(2,1)}, u32[]{:S(2)}) copy-start(bf16[2048,1024]{1,0:T(8,128)(2,1)} %param.3) | copy-start | bytes 12582916
  266.9 53.6 %all-gather.5.cloned.1.call-start = ((), (), s32[]{:S(2)}) async-start(), calls=%async_computation.5 | async-start | bytes 1572864 | tf_op jit(solution)/shard_map/all_gather | solution.py:36
  320.5 16.1 %copy-start.1 = (bf16[2048,1024]{1,0:T(8,128)(2,1)S(1)}, bf16[2048,1024]{1,0:T(8,128)(2,1)}, u32[]{:S(2)}) copy-start(bf16[2048,1024]{1,0:T(8,128)(2,1)} %param.3) | copy-start | bytes 12582916
  320.5 16.1 %copy-start.3 = (f32[1024,256]{1,0:T(8,128)S(1)}, f32[1024,256]{1,0:T(8,128)}, u32[]{:S(2)}) copy-start(f32[1024,256]{1,0:T(8,128)} %all-gather.5.cloned.1.call-done) | copy-start | bytes 3145732
Sparse Core Ops, SparseCore 0:
  9.5 11.7 all-gather.2
  32.4 127.7 all-reduce.3
  166.9 17.4 all-reduce.5
  267.0 9.5 reduce-scatter.1
  278.0 10.2 all-gather.4
where the time goes:
time: 368 us; the launch traced here: 362 us
  waiting for transfers between devices  169 us (46%)
  matrix products  73.1 us (20%)
  other arithmetic  57.7 us (16%)
  blocking collectives  40.8 us (11%)
  between operations  15.5 us (4%)
  local copies, waits for them, and re-layouts  5.14 us (1%)
    psum x1, waiting for transfers between devices, body(): left = lax.psum(partial_value, 'col')  128 us
    psum x1, blocking collectives, body(): squares_right = lax.psum(jnp.sum(share * share, axis=0), ('col', 'row'))  40.8 us
    another operation x6, other arithmetic, body(): lower = jnp.linalg.cholesky(gram)  34 us
    another operation x3, other arithmetic, body(): left_orth = jax.scipy.linalg.solve_triangular(lower, left.T, lower=True).T  19.7 us
    dot_general x1, matrix products, body(): lax.dot_general(left_orth, right_whole, contract_cols, precision=highest,...  18.4 us
    psum x1, waiting for transfers between devices, body(): gram = lax.psum(local_gram, 'row')  17 us
    dot_general x1, matrix products, body(): lax.dot_general(blend, left_orth, contract_rows, precision=highest, prefe...  16.6 us
    dot_general x1, matrix products, body(): lax.dot_general(left_orth, right_unit, contract_cols, precision=highest,...  16.1 us
  transfers between devices with their start and end apart: 5, of which 4 were waited for; matrix products, arithmetic and copies ran while one was open for 1% of the time, Pallas kernels for 0%

commit v1 on v0

--- a/solution.py
+++ b/solution.py
@@ -19,7 +19,10 @@
     partial_value = jnp.dot(
         blend, right_block, precision=highest, preferred_element_type=jnp.float32
     )
-    left = lax.psum(partial_value, "col")
+    n_dev, left = (lax.axis_size("col"), partial_value)
+    for far in [1 << k for k in range(n_dev.bit_length() - 1)]:
+        swap = [(i, i ^ far) for i in range(n_dev)]
+        left = left + lax.ppermute(left, "col", swap)
     local_gram = lax.dot_general(
         left, left, contract_rows, precision=highest, preferred_element_type=jnp.float32
     )

time: 368 us -> 475 us (1.29)
  waiting for transfers between devices: 169 us -> 264 us
  starting transfers between devices: 0.73 us -> 8.83 us
    ppermute x0 -> x4, waiting for transfers between devices: none -> 224 us  [body(): left = left + lax.ppermute(left, 'col', swap)]
    psum x1 -> x0, waiting for transfers between devices: 128 us -> none  [body(): left = lax.psum(partial_value, 'col')]
    ppermute x0 -> x4, starting transfers between devices: none -> 8.14 us  [body(): left = left + lax.ppermute(left, 'col', swap)]
  transfers between devices with their start and end apart: 5 -> 8, of which waited for: 4 -> 7; matrix products, arithmetic and copies ran while one was open for 1% -> 1% of each run, Pallas kernels for 0% -> 0%
where the time goes in v1:
time: 475 us; the launch traced here: 468 us
  waiting for transfers between devices  264 us (56%)
  matrix products  72 us (15%)
  other arithmetic  61.7 us (13%)
  blocking collectives  40.8 us (9%)
  between operations  15.7 us (3%)
  starting transfers between devices  8.83 us (2%)
  local copies, waits for them, and re-layouts  5.07 us (1%)
    ppermute x4, waiting for transfers between devices, body(): left = left + lax.ppermute(left, 'col', swap)  224 us
    psum x1, blocking collectives, body(): squares_right = lax.psum(jnp.sum(share * share, axis=0), ('col', 'row'))  40.8 us
    another operation x6, other arithmetic, body(): lower = jnp.linalg.cholesky(gram)  34 us
    another operation x3, other arithmetic, body(): left_orth = jax.scipy.linalg.solve_triangular(lower, left.T, lower=True).T  19.7 us
    dot_general x1, matrix products, body(): lax.dot_general(left_orth, right_whole, contract_cols, precision=highest,...  18.4 us
    dot_general x1, matrix products, body(): lax.dot_general(blend, left_orth, contract_rows, precision=highest, prefe...  16.6 us
    dot_general x1, matrix products, body(): lax.dot_general(left_orth, right_unit, contract_cols, precision=highest,...  16.1 us
    psum x1, waiting for transfers between devices, body(): gram = lax.psum(local_gram, 'row')  15.8 us
  transfers between devices with their start and end apart: 8, of which 7 were waited for; matrix products, arithmetic and copies ran while one was open for 1% of the time, Pallas kernels for 0%

profile of v1, /device:TPU:0, one launch (start us, length us, event | category | flops | bytes accessed | tf_op | source)
XLA Modules:
  0.0 468.1 jit_solution(8619989926110456937)
XLA Ops:
  7.2 0.0 all-gather.3.cloned.1.call-start
  7.2 0.7 all-gather.3.cloned.1.call-update
  7.9 0.0 all-reduce.3.cloned.1.call-start
  7.9 13.4 %all-gather.3.cloned.1.call-done = f32[1024,256]{1,0:T(8,128)} async-done(((f32[512,256]{1,0:T(8,128)}), f32[1024,256]{1,0:T(8,128)}) %all-gather.3.cloned.1.call-update) | async-done | bytes 1048592 | tf_op jit(solution)/shard_map/all_gather | solution.py:17
  21.3 10.0 %fusion.1 = f32[2048,256]{1,0:T(8,128)S(1)} fusion(f32[1024,256]{1,0:T(8,128)} %all-gather.3.cloned.1.call-done, f32[2048,1024]{1,0:T(8,128)} %param.4, bf16[2048,1024]{1,0:T(8,128)(2,1)} %param.3), kind=kOutput, calls=%fused_computation.6 | convolution fusion | flops 6446645248 | bytes 15728640 | tf_op jit(solution)/shard_map/dot_general | solution.py:19
  31.3 1.8 collective-permute-start
  33.1 46.1 %collective-permute-done = f32[2048,256]{1,0:T(8,128)S(1)} collective-permute-done((f32[2048,256]{1,0:T(8,128)S(1)}, f32[2048,256]{1,0:T(8,128)S(1)}, u32[]{:S(2)}, u32[]{:S(2)}) %collective-permute-start) | collective-permute-done | bytes 2097184 | tf_op jit(solution)/shard_map/ppermute | solution.py:25
  79.2 0.3 add.51
  79.5 1.8 collective-permute-start.1
  81.3 45.2 %collective-permute-done.1 = f32[2048,256]{1,0:T(8,128)S(1)} collective-permute-done((f32[2048,256]{1,0:T(8,128)S(1)}, f32[2048,256]{1,0:T(8,128)S(1)}, u32[]{:S(2)}, u32[]{:S(2)}) %collective-permute-start.1) | collective-permute-done | bytes 2097184 | tf_op jit(solution)/shard_map/ppermute | solution.py:25
  126.5 0.3 add.52
  126.8 1.8 collective-permute-start.2
  128.6 44.4 %collective-permute-done.2 = f32[2048,256]{1,0:T(8,128)S(1)} collective-permute-done((f32[2048,256]{1,0:T(8,128)S(1)}, f32[2048,256]{1,0:T(8,128)S(1)}, u32[]{:S(2)}, u32[]{:S(2)}) %collective-permute-start.2) | collective-permute-done | bytes 2097184 | tf_op jit(solution)/shard_map/ppermute | solution.py:25
  173.0 0.3 add.53
  173.3 2.7 collective-permute-start.3
  176.0 88.6 %collective-permute-done.3 = f32[2048,256]{1,0:T(8,128)} collective-permute-done((f32[2048,256]{1,0:T(8,128)S(1)}, f32[2048,256]{1,0:T(8,128)}, u32[]{:S(2)}, u32[]{:S(2)}) %collective-permute-start.3) | collective-permute-done | bytes 2097184 | tf_op jit(solution)/shard_map/ppermute | solution.py:25
  264.5 6.4 %fusion.6 = f32[256,256]{0,1:T(8,128)} fusion(f32[2048,256]{1,0:T(8,128)S(1)} %add.53, f32[2048,256]{1,0:T(8,128)} %collective-permute-done.3), kind=kOutput, calls=%fused_computation.15 | convolution fusion | flops 1611137024 | bytes 4456448 | tf_op jit(solution)/shard_map/dot_general | solution.py:26
  271.0 0.0 all-reduce.3.cloned.1.call-update
  271.0 0.6 reduce-scatter.2.cloned.1.call-start
  271.6 3.2 add_bitcast_fusion
  274.7 0.0 copy-start.2
  274.7 15.8 %all-reduce.3.cloned.1.call-done = f32[256,256]{0,1:T(8,128)} async-done(((f32[256,256]{0,1:T(8,128)}), f32[256,256]{0,1:T(8,128)}) %all-reduce.3.cloned.1.call-update) | async-done | bytes 262160 | tf_op jit(solution)/shard_map/psum | solution.py:29
  290.5 1.1 copy.7
  291.6 1.0 fusion.9
  292.6 11.7 %cholesky.50 = f32[128,128]{1,0:T(8,128)S(1)} custom-call(f32[128,128]{1,0:T(8,128)S(1)} %cholesky.118), custom_call_target="Cholesky" | custom-call | tf_op jit(solution)/shard_map/jit(cholesky)/cholesky | solution.py:30
  304.3 9.8 %custom-call.15 = f32[1,128,128]{1,2,0:T(8,128)S(1)} custom-call(f32[1,128,128]{2,1,0:T(8,128)S(1)} %get-tuple-element.24), custom_call_target="InvertDiagBlocksLowerTriangular" | custom-call | tf_op jit(solution)/shard_map/jit(cholesky)/cholesky | solution.py:30
  314.2 0.2 constant_dynamic-update-slice_fusion.1
  314.4 0.3 convolution_subtract_fusion
  314.7 11.7 %cholesky.105 = f32[128,128]{1,0:T(8,128)S(1)} custom-call(f32[128,128]{1,0:T(8,128)S(1)} %convolution_subtract_fusion), custom_call_target="Cholesky" | custom-call | tf_op jit(solution)/shard_map/jit(cholesky)/cholesky | solution.py:30
  326.4 0.7 compare_reduce_fusion
  328.4 0.1 triangular_solve.57
  328.5 4.1 while.1
  328.6 0.6 fusion.25
  329.2 1.3 bitcast_dynamic-update-slice_fusion.2
  330.6 0.6 fusion.25
  331.2 1.3 bitcast_dynamic-update-slice_fusion.2
  332.5 19.7 %custom-call.16 = f32[2,128,128]{1,2,0:T(8,128)S(1)} custom-call(f32[2,128,128]{2,1,0:T(8,128)S(1)} %get-tuple-element.10), custom_call_target="InvertDiagBlocksLowerTriangular" | custom-call | tf_op jit(solution)/shard_map/jit(_solve_triangular)/triangular_solve | solution.py:31
  352.2 0.0 copy-done.2
  352.2 0.0 copy-start.3
  352.3 1.1 fusion.3
  353.3 0.0 copy-start
  353.3 1.8 fusion.10
  355.2 0.0 copy-done.3
  355.2 1.1 fusion.2
  356.2 0.0 copy-done
  356.3 16.6 %fusion = f32[1024,256]{1,0:T(8,128)} fusion(f32[2048,1024]{1,0:T(8,128)} %param.4, bf16[2048,1024]{1,0:T(8,128)(2,1)S(1)} %copy-done, f32[128,2048]{1,0:T(8,128)S(1)} %fusion.2, f32[128,2048]{1,0:T(8,128)S(1)} %fusion.3), kind=kOutput, calls=%fused_computation.5 | convolution fusion | flops 6447169536 | bytes 15728640 | tf_op jit(solution)/shard_map/dot_general | solution.py:32
  372.9 0.0 reduce-scatter.2.cloned.1.call-update
  372.9 0.0 all-gather.5.cloned.1.call-start
  373.0 9.7 %reduce-scatter.2.cloned.1.call-done = f32[512,256]{1,0:T(8,128)} async-done(((f32[1024,256]{1,0:T(8,128)}), f32[512,256]{1,0:T(8,128)}) %reduce-scatter.2.cloned.1.call-update) | async-done | bytes 524304 | tf_op jit(solution)/shard_map/reduce_scatter | solution.py:35
  382.7 0.0 all-gather.5.cloned.1.call-update
  382.7 1.1 multiply_reduce_fusion
  383.8 40.8 %psum.15 = f32[256]{0:T(256)S(1)} all-reduce(f32[256]{0:T(256)S(1)} %multiply_reduce_fusion), channel_id=1, replica_groups=mesh['col'=16,'row'=2] {'col','row'}, use_global_device_ids=true, to_apply=%region_7.8 | all-reduce | flops 256 | bytes 2048 | tf_op jit(solution)/shard_map/psum | solution.py:36
  424.6 1.9 broadcast_divide_fusion
  426.5 0.0 all-gather.5.cloned.1.call-done
  426.5 0.0 copy-start.1
  426.5 0.0 copy-start.4
  426.5 16.1 %multiply_convert_fusion = bf16[2048,1024]{1,0:T(8,128)(2,1)} fusion(f32[128,2048]{1,0:T(8,128)S(1)} %fusion.2, f32[128,2048]{1,0:T(8,128)S(1)} %fusion.3, f32[1024,256]{1,0:T(8,128)} %all-gather.5.cloned.1.call-done, f32[256]{0:T(256)S(1)} %add_sqrt_fusion), kind=kOutput, calls=%fused_computation.2 | convolution fusion | flops 6447431680 | bytes 7341056 | tf_op jit(solution)/shard_map/dot_general | solution.py:47
  442.6 0.0 copy-done.1
  442.6 0.0 copy-done.4
  442.6 18.4 %multiply_subtract_fusion = f32[2048,1024]{1,0:T(8,128)} fusion(f32[1024,256]{1,0:T(8,128)S(1)} %copy-done.4, f32[2048,1024]{1,0:T(8,128)} %param.4, bf16[2048,1024]{1,0:T(8,128)(2,1)S(1)} %copy-done.1, f32[128,2048]{1,0:T(8,128)S(1)} %fusion.2, f32[128,2048]{1,0:T(8,128)S(1)} %fusion.3), kind=kOutput, calls=%fused_computation.3 | convolution fusion | flops 6451363840 | bytes 24117248 | tf_op jit(solution)/shard_map/dot_general | solution.py:42
  (10 shorter events, 0.2 us)
Async XLA Ops:
  7.2 14.1 %all-gather.3.cloned.1.call-start = ((), (), s32[]{:S(2)}) async-start(), calls=%async_computation.1 | async-start | bytes 1572864 | tf_op jit(solution)/shard_map/all_gather | solution.py:17
  7.9 282.6 %all-reduce.3.cloned.1.call-start = ((), (), s32[]{:S(2)}) async-start(), calls=%async_computation.2 | async-start | bytes 524288 | tf_op jit(solution)/shard_map/psum | solution.py:29
  31.3 47.9 %collective-permute-start = (f32[2048,256]{1,0:T(8,128)S(1)}, f32[2048,256]{1,0:T(8,128)S(1)}, u32[]{:S(2)}, u32[]{:S(2)}) collective-permute-start(f32[2048,256]{1,0:T(8,128)S(1)} %fusion.1), channel_id=1, source_target_pairs={{0,2},{2,0},{4,6},{6,4},{8,10},{10,8},{12,14},{14,12},{16,18},{18,... | collective-permute-start | bytes 6291464 | tf_op jit(solution)/shard_map/ppermute | solution.py:25
  79.5 47.0 %collective-permute-start.1 = (f32[2048,256]{1,0:T(8,128)S(1)}, f32[2048,256]{1,0:T(8,128)S(1)}, u32[]{:S(2)}, u32[]{:S(2)}) collective-permute-start(f32[2048,256]{1,0:T(8,128)S(1)} %add.51), channel_id=1, source_target_pairs={{0,4},{2,6},{4,0},{6,2},{8,12},{10,14},{12,8},{14,10},{16,20},{18,... | collective-permute-start | bytes 6291464 | tf_op jit(solution)/shard_map/ppermute | solution.py:25
  126.8 46.2 %collective-permute-start.2 = (f32[2048,256]{1,0:T(8,128)S(1)}, f32[2048,256]{1,0:T(8,128)S(1)}, u32[]{:S(2)}, u32[]{:S(2)}) collective-permute-start(f32[2048,256]{1,0:T(8,128)S(1)} %add.52), channel_id=1, source_target_pairs={{0,8},{2,10},{4,12},{6,14},{8,0},{10,2},{12,4},{14,6},{16,24},{18,... | collective-permute-start | bytes 6291464 | tf_op jit(solution)/shard_map/ppermute | solution.py:25
  173.3 91.3 %collective-permute-start.3 = (f32[2048,256]{1,0:T(8,128)S(1)}, f32[2048,256]{1,0:T(8,128)}, u32[]{:S(2)}, u32[]{:S(2)}) collective-permute-start(f32[2048,256]{1,0:T(8,128)S(1)} %add.53), channel_id=1, source_target_pairs={{0,16},{2,18},{4,20},{6,22},{8,24},{10,26},{12,28},{14,30},{16,0},... | collective-permute-start | bytes 6291464 | tf_op jit(solution)/shard_map/ppermute | solution.py:25
  271.0 111.7 %reduce-scatter.2.cloned.1.call-start = ((), (), s32[]{:S(2)}) async-start(), calls=%async_computation.3 | async-start | bytes 1572864 | tf_op jit(solution)/shard_map/reduce_scatter | solution.py:35
  274.7 77.5 %copy-start.2 = (f32[256,2048]{0,1:T(8,128)S(1)}, f32[256,2048]{0,1:T(8,128)}, u32[]{:S(2)}) copy-start(f32[256,2048]{0,1:T(8,128)} %add_bitcast_fusion) | copy-start | bytes 6291460
  352.2 2.9 copy-start.3
  353.3 2.9 copy-start
  372.9 53.6 %all-gather.5.cloned.1.call-start = ((), (), s32[]{:S(2)}) async-start(), calls=%async_computation.4 | async-start | bytes 1572864 | tf_op jit(solution)/shard_map/all_gather | solution.py:39
  426.5 16.1 %copy-start.1 = (bf16[2048,1024]{1,0:T(8,128)(2,1)S(1)}, bf16[2048,1024]{1,0:T(8,128)(2,1)}, u32[]{:S(2)}) copy-start(bf16[2048,1024]{1,0:T(8,128)(2,1)} %param.3) | copy-start | bytes 12582916
  426.5 16.1 %copy-start.4 = (f32[1024,256]{1,0:T(8,128)S(1)}, f32[1024,256]{1,0:T(8,128)}, u32[]{:S(2)}) copy-start(f32[1024,256]{1,0:T(8,128)} %all-gather.5.cloned.1.call-done) | copy-start | bytes 3145732
Sparse Core Ops, SparseCore 0:
  9.5 11.7 all-gather.2
  271.1 19.3 all-reduce.2
  373.0 9.5 reduce-scatter.1
  384.1 10.2 all-gather.4
